TPU v7x, 32 devices: a whole 2x2x4 slice. The times are simulated.
32 devices in a mesh: grp: 2 (over core), dp: 4 (over z), mp: 4 (over y, x).
Axes of the slice: x: 2, y: 2, z: 4, core: 2. Of those that a mesh axis runs over, the one named last changes fastest.
Arguments:
- hidden: bfloat16 [1024, 5120], P(('dp', 'mp')), may hold values from -6 to 6
- enc_weight: bfloat16 [5120, 8192], P(None, 'mp'), may hold values from -0.078125 to 0.078125
- enc_bias: bfloat16 [8192], P('mp'), may hold values from -5 to 5
- enc_frozen: bfloat16 [5120, 64], replicated, may hold values from -0.078125 to 0.078125
- enc_adapter: bfloat16 [64, 8192], P(None, 'mp'), may hold values from -0.75 to 0.75
- text_rows: bfloat16 [2560, 8192], P(('dp', 'mp')), may hold values from -6 to 6
- norm_gain: bfloat16 [8192], replicated, may hold values from 0.5 to 1.5
- value_weight: bfloat16 [8192, 1024], P(('dp', 'mp')), may hold values from -0.0625 to 0.0625
- value_bias: bfloat16 [1024], replicated, may hold values from -5 to 5
- llm_frozen: bfloat16 [8192, 64], P(('dp', 'mp')), may hold values from -0.0625 to 0.0625
- llm_adapter: bfloat16 [64, 1024], replicated, may hold values from -0.75 to 0.75
- targets: bfloat16 [2560, 1024], P(('dp', 'mp')), may hold values from -6 to 6
- dest_owner: int32 [1024, 1], replicated, may hold values from 0 to 15; in each aligned block of 256 rows (0 to 255, 256 to 511, ...) at most 32 rows name the same one
- seq_length: int32 [16], P(('dp', 'mp')), may hold values from 128 to 160
Outputs:
- grad_enc: float32 [64, 8192], P('grp', 'mp')
- grad_llm: float32 [64, 1024], P('grp')
Inputs may be any that keep to these rules, and one draw needn't show every extreme that they name: `dest_owner`: within the tokens of one encoder block (aligned blocks of 256 rows) no LLM device is named more than 32 times, and some device is named exactly 32 times in some blocks.
All inputs are finite; a program needn't handle non-finite values.
Results may differ from a plain program's by a relative error of at most 0.003.
Values may be sent and summed in bfloat16 or wider, within the bound.
A program may use at most 128 MiB of HBM per device.

v0:
```python
import jax
import jax.numpy as jnp
from jax import lax
from jax.sharding import PartitionSpec as P

ENC_DEV = 256


epsilon = 1e-06


def passed_along(value, axis, steps):
    count = lax.axis_size(axis)
    first, last = (max(0, -steps), min(count, count - steps))
    return lax.ppermute(value, axis, [(source, source + steps) for source in range(first, last)])


def swapped(array, axis, bit):
    return lax.ppermute(array, axis, [(i, i ^ 1 << bit) for i in range(lax.axis_size(axis))])


def slot_ranks(destiny, owners):
    markers = (destiny[:, None] == jnp.arange(owners, dtype=jnp.int32)[None, :]).astype(jnp.int32)
    return jnp.sum((jnp.cumsum(markers, axis=0) - markers) * markers, axis=1)


def body(
    hidden,
    enc_weight,
    enc_bias,
    enc_frozen,
    enc_adapter,
    text_rows,
    norm_gain,
    value_weight,
    value_bias,
    llm_frozen,
    llm_adapter,
    targets,
    dest_owner,
    seq_length,
):
    data_ways = lax.axis_size("dp")
    model_ways = lax.axis_size("mp")
    owners = data_ways * model_ways
    capacity = 2 * ENC_DEV // owners
    area = capacity * data_ways
    encoder = lax.axis_index("grp") == 0
    data_index = lax.axis_index("dp")
    owner_index = data_index * model_ways + lax.axis_index("mp")
    part_width = enc_weight.shape[1]
    rank_width = enc_frozen.shape[1]
    kv_width = llm_adapter.shape[1]
    group_rows = lax.all_gather(hidden, "mp", axis=0, tiled=True)

    def encode(source):
        low_rank = jnp.dot(source, enc_frozen, preferred_element_type=jnp.float32).astype(
            jnp.bfloat16
        )
        merged = jnp.dot(source, enc_weight, preferred_element_type=jnp.float32) + enc_bias.astype(
            jnp.float32
        )
        merged = merged + jnp.dot(low_rank, enc_adapter, preferred_element_type=jnp.float32)
        return (merged.astype(jnp.bfloat16), low_rank)

    def rest_encode(source):
        return (
            jnp.zeros((source.shape[0], part_width), jnp.bfloat16),
            jnp.zeros((source.shape[0], rank_width), jnp.bfloat16),
        )

    merged_rows, enc_low = lax.cond(encoder, encode, rest_encode, group_rows)
    destiny = dest_owner[:, 0]
    own_dest = lax.dynamic_slice_in_dim(destiny, data_index * ENC_DEV, ENC_DEV)
    bucket_index = slot_ranks(own_dest, owners) * owners + own_dest
    outgoing = (
        jnp.zeros((capacity * owners, part_width), jnp.bfloat16).at[bucket_index].set(merged_rows)
    )
    outgoing = outgoing.reshape(capacity, owners, part_width)
    grouped = lax.all_to_all(outgoing, ("dp", "mp"), split_axis=1, concat_axis=1, tiled=True)
    arrived = passed_along(grouped, "grp", 1)
    counts = jnp.sum((destiny.reshape(data_ways, ENC_DEV) == owner_index).astype(jnp.int32), axis=1)
    usable = (jnp.arange(capacity, dtype=jnp.int32)[:, None] < counts[None, :]).reshape(area, 1)
    gathered = (
        lax.all_gather(value_weight, ("dp", "mp"), axis=0, tiled=True),
        lax.all_gather(llm_frozen, ("dp", "mp"), axis=0, tiled=True),
    )

    def learn_layer(operands):
        incoming, whole_value, whole_frozen = operands
        image_rows = incoming.reshape(area, -1)
        head_rows = jnp.where(usable, image_rows, text_rows[:area])
        all_rows = jnp.concatenate([head_rows, text_rows[area:]], axis=0)
        wide_rows = all_rows.astype(jnp.float32)
        inverse = lax.rsqrt(jnp.mean(wide_rows * wide_rows, axis=1, keepdims=True) + epsilon)
        gain_wide = norm_gain.astype(jnp.float32)
        normed = (wide_rows * inverse * gain_wide).astype(jnp.bfloat16)
        low_rank = jnp.dot(normed, whole_frozen, preferred_element_type=jnp.float32).astype(
            jnp.bfloat16
        )
        values_out = jnp.dot(
            normed, whole_value, preferred_element_type=jnp.float32
        ) + value_bias.astype(jnp.float32)
        values_out = values_out + jnp.dot(low_rank, llm_adapter, preferred_element_type=jnp.float32)
        length = seq_length[0]
        position = jnp.arange(all_rows.shape[0], dtype=jnp.int32)
        row_weight = jnp.where(position < length, 1.0 / length.astype(jnp.float32), 0.0)
        dvalues = ((values_out - targets.astype(jnp.float32)) * row_weight[:, None]).astype(
            jnp.bfloat16
        )
        grad_part = jnp.dot(low_rank.T, dvalues, preferred_element_type=jnp.float32)
        head_dv = dvalues[:area]
        low_grad = jnp.dot(head_dv, llm_adapter.T, preferred_element_type=jnp.float32).astype(
            jnp.bfloat16
        )
        dnormed = jnp.dot(head_dv, whole_value.T, preferred_element_type=jnp.float32)
        dnormed = dnormed + jnp.dot(low_grad, whole_frozen.T, preferred_element_type=jnp.float32)
        scaled = gain_wide * dnormed
        head_wide = wide_rows[:area]
        head_inverse = inverse[:area]
        cubed = head_inverse * head_inverse * head_inverse
        image_grad = head_inverse * scaled - head_wide * cubed * jnp.mean(
            scaled * head_wide, axis=1, keepdims=True
        )
        image_grad = image_grad.astype(jnp.bfloat16)
        reply_rows = jnp.where(usable, image_grad, jnp.zeros_like(image_grad))
        return (grad_part, reply_rows.reshape(capacity, owners, part_width))

    def rest_learn(operands):
        return (
            jnp.zeros((rank_width, kv_width), jnp.float32),
            jnp.zeros((capacity, owners, part_width), jnp.bfloat16),
        )

    llm_part, reply_rows = lax.cond(
        encoder, rest_learn, learn_layer, (arrived, gathered[0], gathered[1])
    )
    llm_total = lax.psum(llm_part, ("dp", "mp"))
    grouped_back = lax.all_to_all(reply_rows, ("dp", "mp"), split_axis=1, concat_axis=1, tiled=True)
    returned = passed_along(grouped_back, "grp", -1)

    def adapt_grad(operands):
        back_rows, low_rank = operands
        image_grad = back_rows.reshape(capacity * owners, part_width)[bucket_index]
        return jnp.dot(low_rank.T, image_grad, preferred_element_type=jnp.float32)

    def rest_adapt(operands):
        return jnp.zeros((rank_width, part_width), jnp.float32)

    enc_part = lax.cond(encoder, adapt_grad, rest_adapt, (returned, enc_low))
    enc_total = lax.psum(enc_part, "dp")
    half_rank = rank_width // 2
    enc_count = half_rank * part_width
    llm_count = half_rank * kv_width
    span = max(enc_count, llm_count)
    enc_upper = enc_total[half_rank:].reshape(-1)
    llm_lower = jnp.pad(llm_total[:half_rank].reshape(-1), (0, span - llm_count))
    sending = jnp.where(encoder, enc_upper, llm_lower)
    received = swapped(sending, "grp", 0)
    grad_enc = jnp.where(encoder, enc_total[:half_rank], received.reshape(half_rank, part_width))
    grad_llm = jnp.where(
        encoder, received[:llm_count].reshape(half_rank, kv_width), llm_total[half_rank:]
    )
    return (grad_enc, grad_llm)


def solution(mesh):
    return jax.shard_map(
        body,
        mesh=mesh,
        in_specs=(
            P(("dp", "mp"), None),
            P(None, "mp"),
            P("mp"),
            P(),
            P(None, "mp"),
            P(("dp", "mp"), None),
            P(),
            P(("dp", "mp"), None),
            P(),
            P(("dp", "mp"), None),
            P(),
            P(("dp", "mp"), None),
            P(),
            P(("dp", "mp")),
        ),
        out_specs=(P("grp", "mp"), P("grp", None)),
        check_vma=False,
    )
```

profile of v0, /device:TPU:0, one launch (start us, length us, event | category | flops | bytes accessed | tf_op | source)
XLA Modules:
  0.0 564.6 jit_solution(298686897474769356)
XLA Ops:
  7.9 1.6 copy.49
  12.6 39.5 %all-gather.4.cloned.1.call-done = bf16[256,5120]{1,0:T(8,128)(2,1)} async-done(((bf16[64,5120]{1,0:T(8,128)(2,1)}), bf16[256,5120]{1,0:T(8,128)(2,1)}) %all-gather.4.cloned.1.call-update) | async-done | bytes 2621456 | tf_op jit(solution)/shard_map/all_gather | solution.py:54
  52.1 15.1 %conditional.3 = (bf16[256,2048]{1,0:T(8,128)(2,1)S(1)}, bf16[256,64]{0,1:T(8,128)(2,1)}) conditional(s32[]{:T(128)} %convert_element_type.60, () %tuple.31, (bf16[256,5120]{1,0:T(8,128)(2,1)}, bf16[5120,2048]{1,0:T(8,128)(2,1)}, bf16[2048]{0:T(1024)(128)(2,1)}, bf16[5120,64]{0,1:T(8,128)(2,1)}, bf16[64,2048]{1,0:T(8,128)(2,1)}) %tuple.32), branch_computations={%region_3.4_spmd, %region_4.5_spmd} | conditional | flops 5605181440 | bytes 44011620 | solution.py:72
  52.1 3.6 convolution_convert_fusion
  55.7 1.2 fusion.21
  56.9 10.3 %fusion.1 = bf16[256,2048]{1,0:T(8,128)(2,1)S(1)} fusion(f32[256,2048]{1,0:T(8,128)S(1)} %fusion.21, bf16[256,5120]{1,0:T(8,128)(2,1)S(1)} %copy-done.1, bf16[5120,2048]{1,0:T(8,128)(2,1)} %get-tuple-element.87, f32[2048]{0:T(1024)S(1)} %convert_element_type.42), kind=kOutput, calls=%fused_computation.4 | convolution fusion | flops 5370281984 | bytes 26746880 | tf_op jit(solution)/shard_map/cond/branch_1_fun/dot_general | solution.py:60
  68.2 3.5 scatter_custom_fusion
  71.7 1.2 copy.48
  72.9 59.7 %all_to_all.10 = bf16[32,16,2048]{2,0,1:T(8,128)(2,1)} all-to-all(bf16[32,16,2048]{2,0,1:T(8,128)(2,1)S(1)} %copy.48), channel_id=1, replica_groups=mesh['grp'=2,'dp'=4,'mp'=4] {'dp','mp'}, dimensions={1} | all-to-all | bytes 4194304 | tf_op jit(solution)/shard_map/all_to_all | solution.py:80
  132.6 1.4 collective-permute-start
  134.1 3.8 collective-permute-done
  137.9 183.1 %all-gather.8.cloned.1.call-done = bf16[8192,1024]{1,0:T(8,128)(2,1)} async-done(((bf16[512,1024]{1,0:T(8,128)(2,1)}), bf16[8192,1024]{1,0:T(8,128)(2,1)}) %all-gather.8.cloned.1.call-update) | async-done | bytes 16777232 | tf_op jit(solution)/shard_map/all_gather | solution.py:85
  321.6 1.2 copy.51
  322.8 31.6 %all_to_all.11 = bf16[32,16,2048]{2,0,1:T(8,128)(2,1)} all-to-all(bf16[32,16,2048]{2,0,1:T(8,128)(2,1)S(1)} %copy.51), channel_id=1, replica_groups=mesh['grp'=2,'dp'=4,'mp'=4] {'dp','mp'}, dimensions={1} | all-to-all | bytes 4194304 | tf_op jit(solution)/shard_map/all_to_all | solution.py:139
  354.3 1.3 collective-permute-start.1
  355.7 56.2 %collective-permute-done.1 = bf16[32,16,2048]{2,0,1:T(8,128)(2,1)S(1)} collective-permute-done((bf16[32,16,2048]{2,0,1:T(8,128)(2,1)}, bf16[32,16,2048]{2,0,1:T(8,128)(2,1)S(1)}, u32[]{:S(2)}, u32[]{:S(2)}) %collective-permute-start.1) | collective-permute-done | bytes 2097184 | tf_op jit(solution)/shard_map/ppermute | solution.py:15
  411.9 6.5 %conditional.5 = (f32[64,2048]{1,0:T(8,128)S(1)}) conditional(s32[]{:T(128)} %convert_element_type.60, () %tuple.30, (bf16[32,16,2048]{2,0,1:T(8,128)(2,1)S(1)}, s32[256]{0:T(256)S(1)}, s32[256]{0:T(256)S(1)}, bf16[256,64]{0,1:T(8,128)(2,1)}) %tuple.70), branch_computations={%region_11.12_spmd, %region_12.13_spmd} | conditional | flops 67111168 | bytes 16294948 | solution.py:150
  411.9 1.3 copy-done.3
  413.3 2.7 copy.52
  416.0 1.4 gather_fusion
  417.4 1.1 convolution_bitcast_fusion
  419.3 94.8 %all-reduce.6.cloned.1.call-done = f32[64,1024]{1,0:T(8,128)} async-done(((f32[64,1024]{1,0:T(8,128)}), f32[64,1024]{1,0:T(8,128)}) %all-reduce.6.cloned.1.call-update) | async-done | bytes 262160 | tf_op jit(solution)/shard_map/psum | solution.py:138
  515.1 38.7 %all-reduce.4.cloned.1.call-done = f32[64,2048]{1,0:T(8,128)} async-done(((f32[64,2048]{1,0:T(8,128)}), f32[64,2048]{1,0:T(8,128)}) %all-reduce.4.cloned.1.call-update) | async-done | bytes 524304 | tf_op jit(solution)/shard_map/psum | solution.py:151
  555.0 1.5 collective-permute-done.2
  (65 shorter events, 10.2 us)
Async XLA Ops:
  7.2 44.9 %all-gather.4.cloned.1.call-start = ((), (), s32[]{:S(2)}) async-start(), calls=%async_computation.2 | async-start | bytes 3276800 | tf_op jit(solution)/shard_map/all_gather | solution.py:54
  7.9 126.2 %all-gather.6.cloned.1.call-start = ((), (), s32[]{:S(2)}) async-start(), calls=%async_computation.3 | async-start | bytes 2228224 | tf_op jit(solution)/shard_map/all_gather | solution.py:86
  9.6 311.5 %all-gather.8.cloned.1.call-start = ((), (), s32[]{:S(2)}) async-start(), calls=%async_computation.4 | async-start | bytes 17825792 | tf_op jit(solution)/shard_map/all_gather | solution.py:85
  10.3 503.8 %all-reduce.6.cloned.1.call-start = ((), (), s32[]{:S(2)}) async-start(), calls=%async_computation.6 | async-start | bytes 524288 | tf_op jit(solution)/shard_map/psum | solution.py:138
  52.1 3.6 copy-start.11
  52.1 4.8 copy-start.15
  52.1 4.8 copy-start.1
  67.2 1.0 copy-start.6
  72.9 248.2 %copy-start.8 = (bf16[64,1024]{1,0:T(8,128)(2,1)S(1)}, bf16[64,1024]{1,0:T(8,128)(2,1)}, u32[]{:S(2)}) copy-start(bf16[64,1024]{1,0:T(8,128)(2,1)} %param.30) | copy-start | bytes 393220
  72.9 248.2 %copy-start.10 = (bf16[160,1024]{1,0:T(8,128)(2,1)S(1)}, bf16[160,1024]{1,0:T(8,128)(2,1)}, u32[]{:S(2)}) copy-start(bf16[160,1024]{1,0:T(8,128)(2,1)} %param.31) | copy-start | bytes 983044
  72.9 248.2 %copy-start.13 = (bf16[8192]{0:T(1024)(128)(2,1)S(1)}, bf16[8192]{0:T(1024)(128)(2,1)}, u32[]{:S(2)}) copy-start(bf16[8192]{0:T(1024)(128)(2,1)} %param.26) | copy-start | bytes 49156
  72.9 248.2 %copy-start.14 = (s32[1024,1]{0,1:T(1,128)S(1)}, s32[1024,1]{0,1:T(1,128)}, u32[]{:S(2)}) copy-start(s32[1024,1]{0,1:T(1,128)} %param.32) | copy-start | bytes 12292
  72.9 248.2 %copy-start.16 = (bf16[1024]{0:T(1024)(128)(2,1)S(1)}, bf16[1024]{0:T(1024)(128)(2,1)}, u32[]{:S(2)}) copy-start(bf16[1024]{0:T(1024)(128)(2,1)} %param.28) | copy-start | bytes 6148
  132.6 5.3 collective-permute-start
  321.6 32.8 %copy-start.7 = (f32[64,1024]{1,0:T(8,128)}, f32[64,1024]{1,0:T(8,128)S(1)}, u32[]{:S(2)}) copy-start(f32[64,1024]{1,0:T(8,128)S(1)} %get-tuple-element.82) | copy-start | bytes 786436
  354.3 57.6 %collective-permute-start.1 = (bf16[32,16,2048]{2,0,1:T(8,128)(2,1)}, bf16[32,16,2048]{2,0,1:T(8,128)(2,1)S(1)}, u32[]{:S(2)}, u32[]{:S(2)}) collective-permute-start(bf16[32,16,2048]{2,0,1:T(8,128)(2,1)} %all_to_all.11), channel_id=1, source_target_pairs={{16,0},{17,1},{18,2},{19,3},{20,4},{21,5},{22,6},{23,7},{24,8},{25... | collective-permute-start | bytes 6291464 | tf_op jit(solution)/shard_map/ppermute | solution.py:15
  355.7 198.1 %all-reduce.4.cloned.1.call-start = ((), (), s32[]{:S(2)}) async-start(), calls=%async_computation.5 | async-start | bytes 1048576 | tf_op jit(solution)/shard_map/psum | solution.py:151
  411.9 1.3 copy-start.3
  418.5 0.8 copy-start.4
  514.1 43.3 %copy-start.12 = (f32[64,1024]{1,0:T(8,128)S(1)}, f32[64,1024]{1,0:T(8,128)}, u32[]{:S(2)}) copy-start(f32[64,1024]{1,0:T(8,128)} %all-reduce.6.cloned.1.call-done) | copy-start | bytes 786436
  553.8 2.8 copy-start.9
  554.9 1.6 collective-permute-start.2
Sparse Core Ops, SparseCore 0:
  9.8 42.2 all-gather.3
  55.5 72.8 all-gather.5
  131.1 189.8 all-gather.7
  355.8 158.2 all-reduce.5
  516.3 37.5 all-reduce.3
where the time goes:
time: 565 us
  waiting for transfers between devices  419 us (74%)
  blocking collectives  91.3 us (16%)
  local copies, waits for them, and re-layouts  18 us (3%)
  matrix products  16.1 us (3%)
  between operations  14 us (2%)
    all_gather x1, waiting for transfers between devices, body(): lax.all_gather(value_weight, ('dp', 'mp'), axis=0, tiled=True)  183 us
    psum x1, waiting for transfers between devices, body(): llm_total = lax.psum(llm_part, ('dp', 'mp'))  94.8 us
    ppermute x2, waiting for transfers between devices, passed_along(): lax.ppermute(value, axis, [(source, source + steps) for source in range(f...  60 us
    all_to_all x1, blocking collectives, body(): lax.all_to_all(outgoing, ('dp', 'mp'), split_axis=1, concat_axis=1, tiled...  59.7 us
    all_gather x1, waiting for transfers between devices, body(): group_rows = lax.all_gather(hidden, 'mp', axis=0, tiled=True)  39.5 us
    psum x1, waiting for transfers between devices, body(): enc_total = lax.psum(enc_part, 'dp')  38.7 us
    all_to_all x1, blocking collectives, body(): lax.all_to_all(reply_rows, ('dp', 'mp'), split_axis=1, concat_axis=1, til...  31.6 us
  transfers between devices with their start and end apart: 8, of which 7 were waited for; matrix products, arithmetic and copies ran while one was open for 5% of the time, Pallas kernels for 0%

commit v1 on v0

v1 whole, which is shorter than its diff:
```python
import jax
import jax.numpy as jnp
from jax import lax
from jax.sharding import PartitionSpec as P

epsilon = 1e-06
F32 = jnp.float32
BF16 = jnp.bfloat16


def swapped(array, axis, bit):
    return lax.ppermute(array, axis, [(i, i ^ 1 << bit) for i in range(lax.axis_size(axis))])


def summed(array, axis):
    for bit in range(lax.axis_size(axis).bit_length() - 1):
        array = array + swapped(array, axis, bit)
    return array


def slot_ranks(destiny, owners):
    markers = (destiny[:, None] == jnp.arange(owners, dtype=jnp.int32)[None, :]).astype(jnp.int32)
    return jnp.sum((jnp.cumsum(markers, axis=0) - markers) * markers, axis=1)


def body(
    hidden,
    enc_weight,
    enc_bias,
    enc_frozen,
    enc_adapter,
    text_rows,
    norm_gain,
    value_weight,
    value_bias,
    llm_frozen,
    llm_adapter,
    targets,
    dest_owner,
    seq_length,
):
    data_ways = lax.axis_size("dp")
    model_ways = lax.axis_size("mp")
    owners = data_ways * model_ways
    core = lax.axis_index("grp")
    lead = core == 0
    block = lax.axis_index("dp")
    member = lax.axis_index("mp")
    owner_index = block * model_ways + member
    own_tokens = hidden.shape[0]
    block_tokens = own_tokens * model_ways
    capacity = 2 * block_tokens // owners
    area = capacity * data_ways
    llm_rows, model_width = text_rows.shape
    rank = enc_frozen.shape[1]
    kv_half = llm_adapter.shape[1] // 2
    col_half = enc_weight.shape[1] // 2

    def half_of(array, axis):
        size = array.shape[axis] // 2
        return lax.dynamic_slice_in_dim(array, core * size, size, axis)

    def in_order(mine, other):
        return jnp.where(lead, mine, other), jnp.where(lead, other, mine)

    part = lax.all_gather(half_of(hidden, 0), "mp", axis=0, tiled=False)
    padding = -(kv_half + rank) % 128
    packed = jnp.concatenate(
        [half_of(value_weight, 1), llm_frozen, jnp.zeros((llm_frozen.shape[0], padding), BF16)],
        axis=1,
    )
    packed, part = lax.optimization_barrier((packed, part))
    weights = lax.all_gather(packed, ("dp", "mp"), axis=0, tiled=True)

    group_rows = jnp.stack(in_order(part, swapped(part, "grp", 0)), axis=1)
    group_rows = group_rows.reshape(block_tokens, hidden.shape[1])
    enc_low = jnp.dot(group_rows, enc_frozen, preferred_element_type=F32).astype(BF16)
    merged = jnp.dot(group_rows, half_of(enc_weight, 1), preferred_element_type=F32)
    merged = merged + half_of(enc_bias, 0).astype(F32)
    merged = merged + jnp.dot(enc_low, half_of(enc_adapter, 1), preferred_element_type=F32)
    merged = merged.astype(BF16).reshape(model_ways, own_tokens, col_half)
    own_cols = lax.all_to_all(merged, "mp", split_axis=0, concat_axis=0, tiled=True)
    first, second = in_order(own_cols, swapped(own_cols, "grp", 0))
    image = jnp.concatenate(
        [piece[k] for k in range(model_ways) for piece in (first, second)], axis=1
    )

    own_targets = half_of(targets, 1)
    head = own_targets[:area].reshape(capacity, data_ways, kv_half)
    head = lax.all_to_all(head, "dp", split_axis=1, concat_axis=1, tiled=True)
    table = lax.all_gather(head, "mp", axis=0, tiled=False)
    table = table.reshape(model_ways * area, kv_half)
    lengths = lax.all_gather(seq_length.astype(F32), ("dp", "mp"), axis=0, tiled=True)
    destiny = dest_owner[:, 0]
    block_dest = lax.dynamic_slice_in_dim(destiny, block * block_tokens, block_tokens)
    block_slot = slot_ranks(block_dest, owners)
    dest = lax.dynamic_slice_in_dim(block_dest, member * own_tokens, own_tokens)
    slot = lax.dynamic_slice_in_dim(block_slot, member * own_tokens, own_tokens)
    index = (dest % model_ways * capacity + slot) * data_ways + dest // model_ways
    picker = (index[:, None] == jnp.arange(model_ways * area, dtype=jnp.int32)[None, :]).astype(BF16)
    image_targets = jnp.dot(picker, table, preferred_element_type=F32)
    owner_marks = dest[:, None] == jnp.arange(owners, dtype=jnp.int32)[None, :]
    image_length = jnp.sum(jnp.where(owner_marks, lengths[None, :], 0.0), axis=1)
    image_place = (slot * data_ways + block).astype(F32)
    image_weight = jnp.where(image_place < image_length, 1.0 / image_length, 0.0)

    counts = jnp.sum(
        (destiny.reshape(data_ways, block_tokens) == owner_index).astype(jnp.int32), axis=1
    )
    position = jnp.arange(llm_rows, dtype=jnp.int32)
    marks = position[:, None] % data_ways == jnp.arange(data_ways, dtype=jnp.int32)[None, :]
    row_count = jnp.sum(jnp.where(marks, counts[None, :], 0), axis=1)
    replaced = (position < area) & (position // data_ways < row_count)
    length = seq_length[0]
    text_weight = jnp.where(
        (position < length) & ~replaced, 1.0 / length.astype(F32), 0.0
    )
    row_weight = jnp.concatenate([image_weight, text_weight])

    gain = norm_gain.astype(F32)

    def norm(rows):
        wide = rows.astype(F32)
        inverse = lax.rsqrt(jnp.mean(wide * wide, axis=1, keepdims=True) + epsilon)
        return (wide * inverse * gain).astype(BF16), inverse

    image_normed, inverse = norm(image)
    text_normed, _ = norm(text_rows)
    normed = jnp.concatenate([image_normed, text_normed], axis=0)
    product = jnp.dot(normed, weights, preferred_element_type=F32)
    low = product[:, kv_half : kv_half + rank].astype(BF16)
    adapter = half_of(llm_adapter, 1)
    values = product[:, :kv_half] + half_of(value_bias, 0).astype(F32)
    values = values + jnp.dot(low, adapter, preferred_element_type=F32)
    all_targets = jnp.concatenate([image_targets, own_targets.astype(F32)], axis=0)
    dvalues = ((values - all_targets) * row_weight[:, None]).astype(BF16)
    grad_llm = jnp.dot(low.T, dvalues, preferred_element_type=F32)

    image_dv = dvalues[:own_tokens]
    dlow = jnp.dot(image_dv, adapter.T, preferred_element_type=F32)
    dlow = (dlow + swapped(dlow, "grp", 0)).astype(BF16)
    dlow = jnp.where(lead, dlow, jnp.zeros_like(dlow))
    sides = jnp.concatenate([image_dv, dlow, jnp.zeros((own_tokens, padding), BF16)], axis=1)
    dnormed = lax.dot_general(
        sides, weights, (((1,), (1,)), ((), ())), preferred_element_type=F32
    )
    pieces = [dnormed[:, k * col_half : (k + 1) * col_half] for k in range(2 * model_ways)]
    even, odd = jnp.stack(pieces[0::2]), jnp.stack(pieces[1::2])
    kept, given = in_order(even, odd)
    dnormed = kept + swapped(given, "grp", 0)
    halves = gain.reshape(model_ways, 2, col_half)
    own_gain = jnp.where(lead, halves[:, 0], halves[:, 1])
    scaled = own_gain[:, None, :] * dnormed
    own_wide = own_cols.astype(F32)
    total = jnp.sum(scaled * own_wide, axis=(0, 2))
    average = ((total + swapped(total, "grp", 0)) / model_width)[None, :, None]
    inv = inverse[None]
    dimage = (inv * scaled - own_wide * (inv * inv * inv) * average).astype(BF16)
    back = lax.all_to_all(dimage, "mp", split_axis=0, concat_axis=0, tiled=True)
    grad_enc = jnp.dot(
        enc_low.T, back.reshape(block_tokens, col_half), preferred_element_type=F32
    )

    grad_llm = summed(grad_llm, "mp")
    grads = summed(jnp.concatenate([grad_enc, grad_llm], axis=1), "dp")
    upper, lower = grads[: rank // 2], grads[rank // 2 :]
    kept, given = in_order(upper, lower)
    first, second = in_order(kept, swapped(given, "grp", 0))
    return (
        jnp.concatenate([first[:, :col_half], second[:, :col_half]], axis=1),
        jnp.concatenate([first[:, col_half:], second[:, col_half:]], axis=1),
    )


def solution(mesh):
    return jax.shard_map(
        body,
        mesh=mesh,
        in_specs=(
            P(("dp", "mp"), None),
            P(None, "mp"),
            P("mp"),
            P(),
            P(None, "mp"),
            P(("dp", "mp"), None),
            P(),
            P(("dp", "mp"), None),
            P(),
            P(("dp", "mp"), None),
            P(),
            P(("dp", "mp"), None),
            P(),
            P(("dp", "mp")),
        ),
        out_specs=(P("grp", "mp"), P("grp", None)),
        check_vma=False,
    )
```

time: 565 us -> 259 us (0.46)
  waiting for transfers between devices: 419 us -> 126 us
  blocking collectives: 91.3 us -> 58.1 us
  starting transfers between devices: 2.96 us -> 16.5 us
  other arithmetic: 2.85 us -> 16.1 us
  local copies, waits for them, and re-layouts: 18 us -> 5.9 us
    all_gather x3 -> x2, waiting for transfers between devices: 223 us -> 63.7 us  [the longest x1 33.7 us: body(): weights = lax.all_gather(packed, ('dp', 'mp'), axis=0, tiled=True)]
    psum x2 -> x0, waiting for transfers between devices: 134 us -> none  [the longest x1 94.8 us: body(): llm_total = lax.psum(llm_part, ('dp', 'mp'))]
    all_to_all x2 -> x0, blocking collectives: 91.3 us -> none  [the longest x1 59.7 us: body(): lax.all_to_all(outgoing, ('dp', 'mp'), split_axis=1, concat_axis=1, tiled...]
    ppermute x2 -> x0, waiting for transfers between devices: 60 us -> none  [passed_along(): lax.ppermute(value, axis, [(source, source + steps) for source in range(f...]
    ppermute x1 -> x10, waiting for transfers between devices: 1.52 us -> 44.1 us  [swapped(): lax.ppermute(array, axis, [(i, i ^ 1 << bit) for i in range(lax.axis_size...]
    unnamed x0 -> x1, blocking collectives: none -> 42.1 us
    all_to_all x0 -> x3, waiting for transfers between devices: none -> 18.5 us  [the longest x1 9.57 us: body(): head = lax.all_to_all(head, 'dp', split_axis=1, concat_axis=1, tiled=True)]
    all_gather x0 -> x1, blocking collectives: none -> 16 us  [body(): table = lax.all_gather(head, 'mp', axis=0, tiled=False)]
  transfers between devices with their start and end apart: 8 -> 15, of which waited for: 7 -> 12; matrix products, arithmetic and copies ran while one was open for 5% -> 9% of each run, Pallas kernels for 0% -> 0%
where the time goes in v1:
time: 259 us; the launch traced here: 258 us
  waiting for transfers between devices  126 us (49%)
  blocking collectives  58.1 us (22%)
  matrix products  20.1 us (8%)
  starting transfers between devices  16.5 us (6%)
  other arithmetic  16.1 us (6%)
  between operations  15.3 us (6%)
  local copies, waits for them, and re-layouts  5.9 us (2%)
    ppermute x10, waiting for transfers between devices, swapped(): lax.ppermute(array, axis, [(i, i ^ 1 << bit) for i in range(lax.axis_size...  44.1 us
    unnamed x1, blocking collectives  42.1 us
    all_gather x1, waiting for transfers between devices, body(): weights = lax.all_gather(packed, ('dp', 'mp'), axis=0, tiled=True)  33.7 us
    all_gather x1, waiting for transfers between devices, body(): part = lax.all_gather(half_of(hidden, 0), 'mp', axis=0, tiled=False)  30 us
    all_gather x1, blocking collectives, body(): table = lax.all_gather(head, 'mp', axis=0, tiled=False)  16 us
    all_to_all x1, waiting for transfers between devices, body(): head = lax.all_to_all(head, 'dp', split_axis=1, concat_axis=1, tiled=True)  9.57 us
    all_to_all x1, waiting for transfers between devices, body(): lax.all_to_all(merged, 'mp', split_axis=0, concat_axis=0, tiled=True)  8.97 us
    dot_general x1, matrix products, body(): product = jnp.dot(normed, weights, preferred_element_type=F32)  7.93 us
  transfers between devices with their start and end apart: 15, of which 12 were waited for; matrix products, arithmetic and copies ran while one was open for 9% of the time, Pallas kernels for 0%

profile of v1, /device:TPU:0, one launch (start us, length us, event | category | flops | bytes accessed | tf_op | source)
XLA Modules:
  0.0 258.4 jit_solution(7647445687864968788)
XLA Ops:
  7.3 1.8 constant_dynamic-slice_fusion.3
  11.3 30.0 %all-gather.7.cloned.1.call-done = bf16[128,5120]{1,0:T(8,128)(2,1)} async-done(((bf16[32,5120]{1,0:T(8,128)(2,1)}), bf16[128,5120]{1,0:T(8,128)(2,1)}) %all-gather.7.cloned.1.call-update) | async-done | bytes 1310736 | tf_op jit(solution)/shard_map/all_gather | solution.py:66
  45.1 42.1 %all-reduce = f32[16]{0:T(128)S(1)} all-reduce(f32[16]{0:T(128)S(1)} %convert_dynamic-update-slice_fusion), channel_id=1, replica_groups=mesh['grp'=2,'dp'=4,'mp'=4] {'dp','mp'}, use_global_device_ids=true, to_apply=%add | all-reduce | flops 16 | bytes 128
  87.6 2.4 fusion.2
  90.1 4.0 %fusion.4 = bf16[160,8192]{1,0:T(8,128)(2,1)} fusion(bf16[160,8192]{1,0:T(8,128)(2,1)} %param.19, f32[8192]{0:T(1024)S(1)} %convert_element_type.74, f32[160]{0:T(256)S(1)} %add_rsqrt_fusion), kind=kLoop, calls=%fused_computation.6 | loop fusion | flops 5242880 | bytes 5276288 | tf_op jit(solution)/shard_map/convert_element_type | solution.py:125
  96.4 5.8 %fusion.12 = f32[256,1024]{1,0:T(8,128)S(1)} fusion(bf16[256,5120]{1,0:T(8,128)(2,1)S(1)} %bitcast.100, bf16[5120,2048]{1,0:T(8,128)(2,1)} %param.15, s32[]{:T(128)S(6)} %select_n.147, f32[1024]{0:T(1024)S(1)} %dynamic-slice_convert_fusion.1), kind=kOutput, calls=%fused_computation.22 | convolution fusion | flops 2684616704 | bytes 14159876 | tf_op jit(solution)/shard_map/dot_general | solution.py:78
  103.4 3.5 %all-to-all-start = ((bf16[4,64,1024]{2,1,0:T(8,128)(2,1)}), bf16[4,64,1024]{2,1,0:T(8,128)(2,1)S(1)}, u32[]{:S(2)}, u32[]{:S(2)}) async-start(bf16[4,64,1024]{2,1,0:T(8,128)(2,1)} %bitcast.5), calls=%async_computation | async-start | bytes 1048576 | tf_op jit(solution)/shard_map/all_to_all | solution.py:82
  106.9 9.0 %all-to-all-done = bf16[4,64,1024]{2,1,0:T(8,128)(2,1)S(1)} async-done(((bf16[4,64,1024]{2,1,0:T(8,128)(2,1)}), bf16[4,64,1024]{2,1,0:T(8,128)(2,1)S(1)}, u32[]{:S(2)}, u32[]{:S(2)}) %all-to-all-start) | async-done | bytes 524320 | tf_op jit(solution)/shard_map/all_to_all | solution.py:82
  115.9 3.3 %all-to-all-start.1 = ((bf16[32,4,512]{2,0,1:T(8,128)(2,1)}), bf16[32,4,512]{2,0,1:T(8,128)(2,1)S(1)}, u32[]{:S(2)}, u32[]{:S(2)}) async-start(bf16[32,4,512]{2,0,1:T(8,128)(2,1)} %copy.28), calls=%async_computation.1 | async-start | bytes 262144 | tf_op jit(solution)/shard_map/all_to_all | solution.py:90
  119.4 9.6 %all-to-all-done.1 = bf16[32,4,512]{2,0,1:T(8,128)(2,1)S(1)} async-done(((bf16[32,4,512]{2,0,1:T(8,128)(2,1)}), bf16[32,4,512]{2,0,1:T(8,128)(2,1)S(1)}, u32[]{:S(2)}, u32[]{:S(2)}) %all-to-all-start.1) | async-done | bytes 131104 | tf_op jit(solution)/shard_map/all_to_all | solution.py:90
  129.1 16.0 %all-gather.1 = bf16[128,4,512]{2,1,0:T(4,128)(2,1)S(1)} all-gather(bf16[32,4,512]{2,1,0:T(4,128)(2,1)S(1)} %copy.29), channel_id=3, replica_groups=mesh['grp'=2,'dp'=4,'mp'=4] {'mp'}, dimensions={0}, use_global_device_ids=true | all-gather | bytes 655360 | tf_op jit(solution)/shard_map/all_gather | solution.py:91
  146.3 33.7 %all-gather.5.cloned.1.call-done = bf16[8192,640]{1,0:T(8,128)(2,1)} async-done(((bf16[512,640]{1,0:T(8,128)(2,1)}), bf16[8192,640]{1,0:T(8,128)(2,1)}) %all-gather.5.cloned.1.call-update) | async-done | bytes 10485776 | tf_op jit(solution)/shard_map/all_gather | solution.py:73
  180.1 7.9 %fusion.5 = f32[224,640]{1,0:T(8,128)S(1)} fusion(bf16[8192,640]{1,0:T(8,128)(2,1)} %all-gather.5.cloned.1.call-done, bf16[160,8192]{1,0:T(8,128)(2,1)} %fusion.4, bf16[64,8192]{1,0:T(8,128)(2,1)S(1)} %fusion.11), kind=kOutput, calls=%fused_computation.7 | convolution fusion | flops 2356150272 | bytes 14729216 | tf_op jit(solution)/shard_map/dot_general | solution.py:130
  189.7 3.3 %fusion.34 = f32[64,8192]{1,0:T(8,128)S(1)} fusion(bf16[8192,640]{1,0:T(8,128)(2,1)S(1)} %copy-done.2, bf16[64,64]{1,0:T(8,128)(2,1)S(1)} %broadcast.122, bf16[64,64]{1,0:T(8,128)(2,1)S(1)} %fusion.45, bf16[64,512]{1,0:T(8,128)(2,1)S(1)} %slice.134), kind=kOutput, calls=%fused_computation.77 | convolution fusion | flops 671334400 | bytes 12664832 | tf_op jit(solution)/shard_map/dot_general | solution.py:144
  194.6 2.8 %collective-permute-done.3 = f32[4,64,1024]{2,1,0:T(8,128)} collective-permute-done((f32[4,64,1024]{2,1,0:T(8,128)}, f32[4,64,1024]{2,1,0:T(8,128)}, u32[]{:S(2)}, u32[]{:S(2)}) %collective-permute-start.3) | collective-permute-done | bytes 1048608 | tf_op jit(solution)/shard_map/ppermute | solution.py:12
  197.4 1.6 fusion.22
  201.3 3.5 %all-to-all-start.2 = ((bf16[4,64,1024]{2,1,0:T(8,128)(2,1)}), bf16[4,64,1024]{2,1,0:T(8,128)(2,1)S(1)}, u32[]{:S(2)}, u32[]{:S(2)}) async-start(bf16[4,64,1024]{2,1,0:T(8,128)(2,1)} %fusion.21), calls=%async_computation.2 | async-start | bytes 1048576 | tf_op jit(solution)/shard_map/all_to_all | solution.py:159
  205.0 2.0 collective-permute-start.5
  207.0 9.2 %collective-permute-done.5 = f32[64,512]{1,0:T(8,128)S(1)} collective-permute-done((f32[64,512]{1,0:T(8,128)S(1)}, f32[64,512]{1,0:T(8,128)S(1)}, u32[]{:S(2)}, u32[]{:S(2)}) %collective-permute-start.5) | collective-permute-done | bytes 131104 | tf_op jit(solution)/shard_map/ppermute | solution.py:12
  216.2 1.5 collective-permute-start.6
  217.7 3.5 %collective-permute-done.6 = f32[64,512]{1,0:T(8,128)S(1)} collective-permute-done((f32[64,512]{1,0:T(8,128)S(1)}, f32[64,512]{1,0:T(8,128)S(1)}, u32[]{:S(2)}, u32[]{:S(2)}) %collective-permute-start.6) | collective-permute-done | bytes 131104 | tf_op jit(solution)/shard_map/ppermute | solution.py:12
  221.7 9.1 %collective-permute-done.7 = f32[64,1536]{1,0:T(8,128)S(1)} collective-permute-done((f32[64,1536]{1,0:T(8,128)S(1)}, f32[64,1536]{1,0:T(8,128)S(1)}, u32[]{:S(2)}, u32[]{:S(2)}) %collective-permute-start.7) | collective-permute-done | bytes 393248 | tf_op jit(solution)/shard_map/ppermute | solution.py:12
  230.8 1.7 collective-permute-start.8
  232.5 16.0 %collective-permute-done.8 = f32[64,1536]{1,0:T(8,128)S(1)} collective-permute-done((f32[64,1536]{1,0:T(8,128)S(1)}, f32[64,1536]{1,0:T(8,128)S(1)}, u32[]{:S(2)}, u32[]{:S(2)}) %collective-permute-start.8) | collective-permute-done | bytes 393248 | tf_op jit(solution)/shard_map/ppermute | solution.py:12
  (122 shorter events, 19.9 us)
Async XLA Ops:
  7.2 36.6 %copy-start.12 = (u32[32]{0:T(128)S(1)}, u32[32]{0:T(128)}, u32[]{:S(2)}) copy-start(u32[32]{0:T(128)} %constant.116) | copy-start | bytes 388
  7.2 34.2 %copy-start.7 = (bf16[8192]{0:T(1024)(128)(2,1)S(1)}, bf16[8192]{0:T(1024)(128)(2,1)}, u32[]{:S(2)}) copy-start(bf16[8192]{0:T(1024)(128)(2,1)} %param.20) | copy-start | bytes 49156
  7.2 34.2 %copy-start.9 = (s32[1024,1]{0,1:T(1,128)S(1)}, s32[1024,1]{0,1:T(1,128)}, u32[]{:S(2)}) copy-start(s32[1024,1]{0,1:T(1,128)} %param.26) | copy-start | bytes 12292
  7.2 35.8 %copy-start.5 = (bf16[160,1024]{1,0:T(8,128)(2,1)S(1)}, bf16[160,1024]{1,0:T(8,128)(2,1)}, u32[]{:S(2)}) copy-start(bf16[160,1024]{1,0:T(8,128)(2,1)} %param.25) | copy-start | bytes 983044
  7.2 34.1 %all-gather.7.cloned.1.call-start = ((), (), s32[]{:S(2)}) async-start(), calls=%async_computation.4 | async-start | bytes 1638400 | tf_op jit(solution)/shard_map/all_gather | solution.py:66
  7.3 80.1 %copy-start.11 = (bf16[1024]{0:T(1024)(128)(2,1)S(1)}, bf16[1024]{0:T(1024)(128)(2,1)}, u32[]{:S(2)}) copy-start(bf16[1024]{0:T(1024)(128)(2,1)} %param.22) | copy-start | bytes 6148
  7.3 80.1 %copy-start.10 = (bf16[2048]{0:T(1024)(128)(2,1)S(1)}, bf16[2048]{0:T(1024)(128)(2,1)}, u32[]{:S(2)}) copy-start(bf16[2048]{0:T(1024)(128)(2,1)} %param.16) | copy-start | bytes 12292
  9.1 170.9 %all-gather.5.cloned.1.call-start = ((), (), s32[]{:S(2)}) async-start(), calls=%async_computation.3 | async-start | bytes 11141120 | tf_op jit(solution)/shard_map/all_gather | solution.py:73
  41.3 48.7 %copy-start.3 = (bf16[128,5120]{1,0:T(8,128)(2,1)S(1)}, bf16[128,5120]{1,0:T(8,128)(2,1)}, u32[]{:S(2)}) copy-start(bf16[128,5120]{1,0:T(8,128)(2,1)} %all-gather.7.cloned.1.call-done) | copy-start | bytes 3932164
  90.0 4.1 %collective-permute-start = (bf16[4,32,5120]{2,1,0:T(8,128)(2,1)S(1)}, bf16[4,32,5120]{2,1,0:T(8,128)(2,1)S(1)}, u32[]{:S(2)}, u32[]{:S(2)}) collective-permute-start(bf16[4,32,5120]{2,1,0:T(8,128)(2,1)S(1)} %bitcast.102), channel_id=1, source_target_pairs={{0,16},{16,0},{1,17},{17,1},{2,18},{18,2},{3,19},{19,3},{4,20},{20... | collective-permute-start | bytes 3932168 | tf_op jit(solution)/shard_map/ppermute | solution.py:12
  103.4 12.5 %all-to-all-start = ((bf16[4,64,1024]{2,1,0:T(8,128)(2,1)}), bf16[4,64,1024]{2,1,0:T(8,128)(2,1)S(1)}, u32[]{:S(2)}, u32[]{:S(2)}) async-start(bf16[4,64,1024]{2,1,0:T(8,128)(2,1)} %bitcast.5), calls=%async_computation | async-start | bytes 1048576 | tf_op jit(solution)/shard_map/all_to_all | solution.py:82
  115.9 13.1 %all-to-all-start.1 = ((bf16[32,4,512]{2,0,1:T(8,128)(2,1)}), bf16[32,4,512]{2,0,1:T(8,128)(2,1)S(1)}, u32[]{:S(2)}, u32[]{:S(2)}) async-start(bf16[32,4,512]{2,0,1:T(8,128)(2,1)} %copy.28), calls=%async_computation.1 | async-start | bytes 262144 | tf_op jit(solution)/shard_map/all_to_all | solution.py:90
  119.2 26.2 %collective-permute-start.1 = (bf16[4,64,1024]{2,1,0:T(8,128)(2,1)S(1)}, bf16[4,64,1024]{2,1,0:T(8,128)(2,1)S(1)}, u32[]{:S(2)}, u32[]{:S(2)}) collective-permute-start(bf16[4,64,1024]{2,1,0:T(8,128)(2,1)S(1)} %all-to-all-done), channel_id=1, source_target_pairs={{0,16},{16,0},{1,17},{17,1},{2,18},{18,2},{3,19},{19,3},{4,20},{20... | collective-permute-start | bytes 1572872 | tf_op jit(solution)/shard_map/ppermute | solution.py:12
  146.3 41.7 %copy-start.8 = (bf16[64,1024]{1,0:T(8,128)(2,1)S(1)}, bf16[64,1024]{1,0:T(8,128)(2,1)}, u32[]{:S(2)}) copy-start(bf16[64,1024]{1,0:T(8,128)(2,1)} %param.24) | copy-start | bytes 393220
  188.4 1.3 collective-permute-start.2
  194.4 3.0 %collective-permute-start.3 = (f32[4,64,1024]{2,1,0:T(8,128)}, f32[4,64,1024]{2,1,0:T(8,128)}, u32[]{:S(2)}, u32[]{:S(2)}) collective-permute-start(f32[4,64,1024]{2,1,0:T(8,128)} %fusion.23), channel_id=1, source_target_pairs={{0,16},{16,0},{1,17},{17,1},{2,18},{18,2},{3,19},{19,3},{4,20},{20... | collective-permute-start | bytes 3145736 | tf_op jit(solution)/shard_map/ppermute | solution.py:12
  199.0 1.2 collective-permute-start.4
  201.3 20.0 %all-to-all-start.2 = ((bf16[4,64,1024]{2,1,0:T(8,128)(2,1)}), bf16[4,64,1024]{2,1,0:T(8,128)(2,1)S(1)}, u32[]{:S(2)}, u32[]{:S(2)}) async-start(bf16[4,64,1024]{2,1,0:T(8,128)(2,1)} %fusion.21), calls=%async_computation.2 | async-start | bytes 1048576 | tf_op jit(solution)/shard_map/all_to_all | solution.py:159
  205.0 11.2 %collective-permute-start.5 = (f32[64,512]{1,0:T(8,128)S(1)}, f32[64,512]{1,0:T(8,128)S(1)}, u32[]{:S(2)}, u32[]{:S(2)}) collective-permute-start(f32[64,512]{1,0:T(8,128)S(1)} %fusion.44), channel_id=1, source_target_pairs={{0,1},{1,0},{2,3},{3,2},{4,5},{5,4},{6,7},{7,6},{8,9},{9,8},{10,11... | collective-permute-start | bytes 393224 | tf_op jit(solution)/shard_map/ppermute | solution.py:12
  216.2 5.0 %collective-permute-start.6 = (f32[64,512]{1,0:T(8,128)S(1)}, f32[64,512]{1,0:T(8,128)S(1)}, u32[]{:S(2)}, u32[]{:S(2)}) collective-permute-start(f32[64,512]{1,0:T(8,128)S(1)} %add.157), channel_id=1, source_target_pairs={{0,2},{1,3},{2,0},{3,1},{4,6},{5,7},{6,4},{7,5},{8,10},{9,11},{10,... | collective-permute-start | bytes 393224 | tf_op jit(solution)/shard_map/ppermute | solution.py:12
  221.5 30.1 %copy-start.1 = (bf16[512,1024]{1,0:T(8,128)(2,1)S(1)}, bf16[512,1024]{1,0:T(8,128)(2,1)}, u32[]{:S(2)}) copy-start(bf16[512,1024]{1,0:T(8,128)(2,1)} %param.21) | copy-start | bytes 3145732
  221.5 9.2 %collective-permute-start.7 = (f32[64,1536]{1,0:T(8,128)S(1)}, f32[64,1536]{1,0:T(8,128)S(1)}, u32[]{:S(2)}, u32[]{:S(2)}) collective-permute-start(f32[64,1536]{1,0:T(8,128)S(1)} %pad_maximum_fusion.3), channel_id=1, source_target_pairs={{0,4},{4,0},{8,12},{12,8},{1,5},{5,1},{9,13},{13,9},{2,6},{6,2},{1... | collective-permute-start | bytes 1179656 | tf_op jit(solution)/shard_map/ppermute | solution.py:12
  230.8 17.7 %collective-permute-start.8 = (f32[64,1536]{1,0:T(8,128)S(1)}, f32[64,1536]{1,0:T(8,128)S(1)}, u32[]{:S(2)}, u32[]{:S(2)}) collective-permute-start(f32[64,1536]{1,0:T(8,128)S(1)} %fusion.63), channel_id=1, source_target_pairs={{0,8},{4,12},{8,0},{12,4},{1,9},{5,13},{9,1},{13,5},{2,10},{6,14},... | collective-permute-start | bytes 1179656 | tf_op jit(solution)/shard_map/ppermute | solution.py:12
  248.6 1.5 collective-permute-start.9
  (4 other events, 19.6 us)
Sparse Core Ops, SparseCore 0:
  9.9 31.3 all-gather.6
  44.0 136.0 all-gather.4
